TPU v7x, 32 devices: a whole 2x2x4 slice. The times are simulated.
32 devices in a mesh: ctx: 8 (over z, y), head: 4 (over x, core).
Axes of the slice: x: 2, y: 2, z: 4, core: 2. Of those that a mesh axis runs over, the one named last changes fastest.
Arguments:
- queries: bfloat16 [2048, 5120], P('ctx', 'head'), parts along dimension 1, may hold values from -6 to 6
- query_tangents: bfloat16 [2048, 5120], P('ctx', 'head'), parts along dimension 1, may hold values from -6 to 6
- keys: bfloat16 [2048, 5120], P('ctx', 'head'), parts along dimension 1, may hold values from -6 to 6
- key_tangents: bfloat16 [2048, 5120], P('ctx', 'head'), parts along dimension 1, may hold values from -6 to 6
- values: bfloat16 [2048, 5120], P('ctx', 'head'), parts along dimension 1, may hold values from -6 to 6
- value_tangents: bfloat16 [2048, 5120], P('ctx', 'head'), parts along dimension 1, may hold values from -6 to 6
- selection: int32 [16, 14], P('ctx'), may hold values from 0 to 1, as said below
Outputs:
- attention_out: bfloat16 [2048, 5120], P('ctx', 'head'), parts along dimension 1
- attention_tangent: bfloat16 [2048, 5120], P('ctx', 'head'), parts along dimension 1
There are 4 independent parts, one for each index of `head`. A program takes and returns all parts, laid end to end along the dimension named above; an argument that names none is the same for every part. Nothing has to cross between parts.
Inputs may be any that keep to these rules, and one draw needn't show every extreme that they name: `selection`: column 6 + b mod 2 of row b, the query block's own block, is always 1.
All inputs are finite; a program needn't handle non-finite values.
Results may differ from a plain program's by a relative error of at most 0.012.
Values may be sent and summed in bfloat16 or wider, within the bound.
A program may use at most 128 MiB of HBM per device.

v0:
```python
import functools

import jax
import jax.numpy as jnp
from jax import lax
from jax.sharding import PartitionSpec as P
from jax.experimental import pallas as pl
from jax.experimental.pallas import tpu as pltpu

HEADS = 10
HEAD_DIM = 128
BLK = 128
REACH = 3


big_negative = -1e30


def from_behind(array, axis, by):
    devices = lax.axis_size(axis)
    return lax.ppermute(array, axis, [(i, (i + by) % devices) for i in range(devices)])


def heads_view(flat_array):
    return flat_array.reshape(flat_array.shape[0], HEADS, HEAD_DIM)


def tile_update(accumulators, query_pieces, key_pieces):
    score_scale = HEAD_DIM ** (-0.5)
    query_block, query_tangent = query_pieces
    key_block, key_tangent, value_block, value_tangent = key_pieces
    running, weight_total, tangent_total, mixed_sum, mixed_tangent = accumulators
    scores = (
        jnp.einsum("qhd,khd->qhk", query_block, key_block, preferred_element_type=jnp.float32)
        * score_scale
    )
    score_tangents = (
        jnp.einsum("qhd,khd->qhk", query_tangent, key_block, preferred_element_type=jnp.float32)
        + jnp.einsum("qhd,khd->qhk", query_block, key_tangent, preferred_element_type=jnp.float32)
    ) * score_scale
    highest = jnp.maximum(running, scores.max(axis=2))
    factor = jnp.exp(running - highest)
    weights = jnp.exp(scores - highest[:, :, None])
    weighted = weights * score_tangents
    weight_total = factor * weight_total + weights.sum(axis=2)
    tangent_total = factor * tangent_total + weighted.sum(axis=2)
    rounded_weights = weights.astype(jnp.bfloat16)
    rounded_tangent = weighted.astype(jnp.bfloat16)
    mixed_sum = factor[:, :, None] * mixed_sum + jnp.einsum(
        "qhk,khd->qhd", rounded_weights, value_block, preferred_element_type=jnp.float32
    )
    mixed_tangent = (
        factor[:, :, None] * mixed_tangent
        + jnp.einsum(
            "qhk,khd->qhd", rounded_tangent, value_block, preferred_element_type=jnp.float32
        )
        + jnp.einsum(
            "qhk,khd->qhd", rounded_weights, value_tangent, preferred_element_type=jnp.float32
        )
    )
    return (highest, weight_total, tangent_total, mixed_sum, mixed_tangent)


def sweep(accumulators, query_pair, chosen_rows, key_pack, column_base):
    per_device = chosen_rows.shape[0]

    def visit(tile_index, carried):
        query_index = tile_index // per_device
        key_index = tile_index % per_device
        picked = chosen_rows[query_index, column_base + key_index] != 0

        def apply(carried_state):
            first_row = query_index * BLK
            pieces = tuple(
                (
                    lax.dynamic_slice_in_dim(full_array, first_row, BLK, 0)
                    for full_array in carried_state
                )
            )
            query_pieces = tuple(
                (
                    lax.dynamic_slice_in_dim(full_array, first_row, BLK, 0)
                    for full_array in query_pair
                )
            )
            key_pieces = tuple(
                (
                    lax.dynamic_slice_in_dim(full_array, key_index * BLK, BLK, 0)
                    for full_array in key_pack
                )
            )
            updated = tile_update(pieces, query_pieces, key_pieces)
            return tuple(
                (
                    lax.dynamic_update_slice_in_dim(full_array, new_piece, first_row, 0)
                    for full_array, new_piece in zip(carried_state, updated)
                )
            )

        return lax.cond(picked, apply, lambda unchanged: unchanged, carried)

    return lax.fori_loop(0, per_device * per_device, visit, tuple(accumulators))


def finish(accumulators):
    running, weight_total, tangent_total, mixed_sum, mixed_tangent = accumulators
    token_count = mixed_sum.shape[0]
    output = mixed_sum / weight_total[:, :, None]
    tangent = (mixed_tangent - output * tangent_total[:, :, None]) / weight_total[:, :, None]
    return (
        output.reshape(token_count, HEADS * HEAD_DIM).astype(jnp.bfloat16),
        tangent.reshape(token_count, HEADS * HEAD_DIM).astype(jnp.bfloat16),
    )


def body(queries, query_tangents, keys, key_tangents, values, value_tangents, selection):
    token_count = queries.shape[0]
    per_device = token_count // BLK
    query_pair = (heads_view(queries), heads_view(query_tangents))
    key_pack = (
        heads_view(keys),
        heads_view(key_tangents),
        heads_view(values),
        heads_view(value_tangents),
    )
    initial = (
        jnp.full((token_count, HEADS), big_negative, jnp.float32),
        jnp.zeros((token_count, HEADS), jnp.float32),
        jnp.zeros((token_count, HEADS), jnp.float32),
        jnp.zeros((token_count, HEADS, HEAD_DIM), jnp.float32),
        jnp.zeros((token_count, HEADS, HEAD_DIM), jnp.float32),
    )
    at_home = sweep(initial, query_pair, selection, key_pack, REACH * per_device)
    accumulators = at_home
    rising = key_pack
    falling = key_pack
    for offset in range(1, REACH + 1):
        rising = from_behind((rising[0], rising[1], rising[2], rising[3]), "ctx", -1)
        accumulators = sweep(
            accumulators, query_pair, selection, rising, (REACH + offset) * per_device
        )
        falling = from_behind((falling[0], falling[1], falling[2], falling[3]), "ctx", 1)
        accumulators = sweep(
            accumulators, query_pair, selection, falling, (REACH - offset) * per_device
        )
    return finish(accumulators)


LOG2E = 1.4426950408889634
MESH = pl.DeviceIdType.MESH


def attend(shard, q_slot, n, q_buf, kv_buf, bias_buf, s_buf):
    scale = HEAD_DIM ** (-0.5)
    factor = scale * LOG2E
    width = 2 * REACH + 1
    d = HEAD_DIM
    both = q_buf[q_slot]
    query = q_buf[q_slot, :, d : 2 * d]
    rows = both.shape[0]
    per_device = rows // BLK
    bias = jnp.where(bias_buf[shard] != 0, 0.0, big_negative)
    dims = (((1,), (1,)), ((), ()))
    slots = [lax.rem(shard + n - REACH + j, n) for j in range(width)]
    high = [None] * per_device
    for j in range(width):
        scores = lax.dot_general(
            query, kv_buf[slots[j], :, 0:d], dims, preferred_element_type=jnp.float32
        )
        for r in range(per_device):
            for k in range(per_device):
                column = j * per_device + k
                there = (slice(r * BLK, (r + 1) * BLK), slice(k * BLK, (k + 1) * BLK))
                masked = scores[there] * factor + bias[r : r + 1, column : column + 1]
                s_buf[(j,) + there] = masked
                high[r] = masked if high[r] is None else jnp.maximum(high[r], masked)
    peak = jnp.concatenate([jnp.max(h, axis=1, keepdims=True) for h in high], axis=0)
    total = jnp.zeros((rows, BLK), jnp.float32)
    tangent_total = jnp.zeros((rows, BLK), jnp.float32)
    mixed = jnp.zeros((rows, 2 * d), jnp.float32)
    mixed_tangent = jnp.zeros((rows, d), jnp.float32)
    for j in range(width):
        tangents = lax.dot_general(
            both, kv_buf[slots[j], :, 0 : 2 * d], dims, preferred_element_type=jnp.float32
        )
        weights = jnp.exp2(s_buf[j] - peak)
        weighted = weights * tangents
        for k in range(per_device):
            lanes = slice(k * BLK, (k + 1) * BLK)
            total = total + weights[:, lanes]
            tangent_total = tangent_total + weighted[:, lanes]
        mixed = mixed + jnp.dot(
            weights.astype(jnp.bfloat16),
            kv_buf[slots[j], :, 2 * d : 4 * d],
            preferred_element_type=jnp.float32,
        )
        mixed_tangent = mixed_tangent + jnp.dot(
            weighted.astype(jnp.bfloat16),
            kv_buf[slots[j], :, 2 * d : 3 * d],
            preferred_element_type=jnp.float32,
        )
    inverse = 1.0 / jnp.sum(total, axis=1, keepdims=True)
    tangent_sum = jnp.sum(tangent_total, axis=1, keepdims=True)
    output = mixed[:, 0:d] * inverse
    tangent = (scale * (mixed_tangent - output * tangent_sum) + mixed[:, d : 2 * d]) * inverse
    return output.astype(jnp.bfloat16), tangent.astype(jnp.bfloat16)


def exchange_kernel(
    n, q_ref, qt_ref, k_ref, kt_ref, v_ref, vt_ref, bias_ref, o_ref, ot_ref,
    q_buf, kv_buf, xq_buf, xkv_buf, bias_buf, out_buf, xout_buf, s_buf,
    kv_send, q_send, b_send, o_send, xkv_send, xq_send, xo_send,
    kv_recv, q_recv, b_recv, o_recv, xkv_recv, xq_recv, xo_recv,
):
    d = HEAD_DIM
    half = n // 2
    extra = HEADS - n
    me = lax.axis_index("ctx")
    side = me // half
    place = lax.rem(me, half)
    first_host = half - extra

    def cols(head):
        return pl.ds(pl.multiple_of(head * d, d), d)

    def host(which_side, e):
        return first_host + which_side * extra + e

    barrier = pltpu.get_barrier_semaphore()
    for i in range(1, n):
        pl.semaphore_signal(
            barrier, inc=1, device_id={"ctx": lax.rem(me + i, n)}, device_id_type=MESH
        )
    pl.semaphore_wait(barrier, n - 1)

    def send(src, dst, send_sem, recv_sem, target):
        pltpu.make_async_remote_copy(
            src_ref=src, dst_ref=dst, send_sem=send_sem, recv_sem=recv_sem,
            device_id={"ctx": target}, device_id_type=MESH,
        ).start()

    def wait(ref, sem):
        pltpu.make_async_copy(ref, ref, sem).wait()

    packs = (k_ref, kt_ref, v_ref, vt_ref)
    pair = (qt_ref, q_ref)

    def lane(i):
        return pl.ds(i * d, d)

    def main_send(refs, buf, send_sem, recv_sem, target):
        for i, ref in enumerate(refs):
            send(ref.at[:, cols(target)], buf.at[me, :, lane(i)], send_sem.at[target], recv_sem.at[me], target)

    def main_keep(refs, buf, recv_sem):
        for i, ref in enumerate(refs):
            pltpu.make_async_copy(ref.at[:, cols(me)], buf.at[me, :, lane(i)], recv_sem.at[me]).start()

    def extra_send(refs, buf, slot, send_sem, recv_sem, which_side, e):
        target = host(which_side, e)

        @pl.when(target != me)
        def _():
            for i, ref in enumerate(refs):
                send(ref.at[:, cols(n + e)], buf.at[slot, :, lane(i)], send_sem, recv_sem.at[slot], target)

        @pl.when(target == me)
        def _():
            for i, ref in enumerate(refs):
                pltpu.make_async_copy(ref.at[:, cols(n + e)], buf.at[slot, :, lane(i)], recv_sem.at[slot]).start()

    across = [(1 - side) * half + lax.rem(place + i, half) for i in range(half)]
    beside = [side * half + lax.rem(place + i, half) for i in range(1, half)]

    turns = [lax.rem(me + e, extra) for e in range(extra)]
    for e in turns:
        extra_send(packs, xkv_buf, me, xkv_send.at[0, e], xkv_recv, 1 - side, e)
    for e in turns:
        extra_send(packs, xkv_buf, me, xkv_send.at[1, e], xkv_recv, side, e)
        extra_send(pair, xq_buf, place, xq_send.at[e], xq_recv, side, e)
    for target in across + beside:
        send(bias_ref, bias_buf.at[me], b_send.at[target], b_recv.at[me], target)
    pltpu.make_async_copy(bias_ref, bias_buf.at[me], b_recv.at[me]).start()
    mixed = [t for two in zip(across, beside) for t in two] + across[len(beside) :]
    for target in mixed:
        main_send(packs, kv_buf, kv_send, kv_recv, target)
    main_keep(packs, kv_buf, kv_recv)
    for target in mixed:
        main_send(pair, q_buf, q_send, q_recv, target)
    main_keep(pair, q_buf, q_recv)

    def each(low, high, step):
        def run(i, carried):
            step(i)
            return carried

        lax.fori_loop(low, high, run, 0)

    each(0, n, lambda i: wait(bias_buf.at[i], b_recv.at[i]))

    is_host = jnp.logical_and(me >= first_host, me < first_host + 2 * extra)
    mine = lax.rem(me - first_host + n * extra, extra)
    outs = (o_ref, ot_ref)

    def put(buf, slot, send_sem, recv_sem, source, head, target):
        @pl.when(target != me)
        def _():
            for i, ref in enumerate(outs):
                send(buf.at[slot, :, lane(i)], ref.at[:, cols(head)], send_sem.at[slot], recv_sem.at[source], target)

        @pl.when(target == me)
        def _():
            for i, ref in enumerate(outs):
                pltpu.make_async_copy(buf.at[slot, :, lane(i)], ref.at[:, cols(head)], recv_sem.at[source]).start()

    @pl.when(is_host)
    def _():
        each(0, n, lambda i: wait(xkv_buf.at[i], xkv_recv.at[i]))
        each(0, half, lambda i: wait(xq_buf.at[i], xq_recv.at[i]))

        def step(i):
            shard = side * half + i
            output, tangent = attend(shard, i, n, xq_buf, xkv_buf, bias_buf, s_buf)
            xout_buf[i, :, 0:d] = output
            xout_buf[i, :, d : 2 * d] = tangent

        each(0, half, step)
        each(0, half, lambda i: put(xout_buf, i, xo_send, xo_recv, mine, n + mine, side * half + i))

    each(0, n, lambda i: wait(kv_buf.at[i], kv_recv.at[i]))

    def order(i):
        turn = i // half
        return lax.rem(side + turn, 2) * half + lax.rem(place + n - i, half)

    def main_step(i):
        shard = order(i)
        wait(q_buf.at[shard], q_recv.at[shard])
        output, tangent = attend(shard, shard, n, q_buf, kv_buf, bias_buf, s_buf)
        out_buf[shard, :, 0:d] = output
        out_buf[shard, :, d : 2 * d] = tangent
        put(out_buf, shard, o_send, o_recv, me, me, shard)

    each(0, n, main_step)

    each(0, n, lambda i: wait(out_buf.at[i], o_recv.at[i]))
    each(0, extra, lambda i: wait(xout_buf.at[i], xo_recv.at[i]))

    def drain(i):
        target = lax.rem(me + i, n)
        wait(kv_buf.at[target], kv_send.at[target])
        wait(q_buf.at[target], q_send.at[target])
        wait(bias_buf.at[target], b_send.at[target])
        wait(out_buf.at[target], o_send.at[target])

    each(1, n, drain)
    for e in range(extra):
        @pl.when(host(1 - side, e) != me)
        def _():
            wait(xkv_buf.at[0], xkv_send.at[0, e])

        @pl.when(host(side, e) != me)
        def _():
            wait(xkv_buf.at[0], xkv_send.at[1, e])
            wait(xq_buf.at[0], xq_send.at[e])

    @pl.when(is_host)
    def _():
        def step(i):
            @pl.when(side * half + i != me)
            def _():
                wait(xout_buf.at[i], xo_send.at[i])

        each(0, half, step)


def exchanged(n, queries, query_tangents, keys, key_tangents, values, value_tangents, selection):
    rows, width = queries.shape
    half, extra, d = n // 2, HEADS - n, HEAD_DIM
    vm = pltpu.VMEM
    dma = pltpu.SemaphoreType.DMA
    reach = 2 * REACH + 1
    bf = jnp.bfloat16
    return pl.pallas_call(
        functools.partial(exchange_kernel, n),
        out_shape=[jax.ShapeDtypeStruct((rows, width), bf)] * 2,
        in_specs=[pl.BlockSpec(memory_space=pl.ANY)] * 7,
        out_specs=[pl.BlockSpec(memory_space=pl.ANY)] * 2,
        scratch_shapes=[
            vm((n, rows, 2 * d), bf),
            vm((n, rows, 4 * d), bf),
            vm((half, rows, 2 * d), bf),
            vm((n, rows, 4 * d), bf),
            vm((n,) + selection.shape, jnp.int32),
            vm((n, rows, 2 * d), bf),
            vm((half, rows, 2 * d), bf),
            vm((reach, rows, rows), jnp.float32),
            dma((n,)), dma((n,)), dma((n,)), dma((n,)), dma((2, extra)), dma((extra,)), dma((half,)),
            dma((n,)), dma((n,)), dma((n,)), dma((n,)), dma((n,)), dma((half,)), dma((extra,)),
        ],
        compiler_params=pltpu.CompilerParams(
            collective_id=0, has_side_effects=True, vmem_limit_bytes=67_043_328
        ),
        name="exchange",
    )(queries, query_tangents, keys, key_tangents, values, value_tangents, selection)


def solution(mesh):
    n = mesh.shape["ctx"]
    covered = n == 2 * REACH + 2 and n < HEADS and 2 * (HEADS - n) <= n
    placed = (
        P("ctx", "head"),
        P("ctx", "head"),
        P("ctx", "head"),
        P("ctx", "head"),
        P("ctx", "head"),
        P("ctx", "head"),
        P("ctx", None),
    )
    return jax.shard_map(
        functools.partial(exchanged, n) if covered else body,
        mesh=mesh,
        in_specs=placed,
        out_specs=(P("ctx", "head"), P("ctx", "head")),
        check_vma=False,
    )
```

profile of v0, /device:TPU:10, one launch (start us, length us, event | category | flops | bytes accessed | tf_op | source)
XLA Modules:
  0.0 125.5 jit_solution(1577108250125996787)
XLA Ops:
  0.6 121.9 %exchange.1 = (bf16[256,1280]{1,0:T(8,128)(2,1)}, bf16[256,1280]{1,0:T(8,128)(2,1)}) custom-call(bf16[256,1280]{1,0:T(8,128)(2,1)} %q_ref.1, bf16[256,1280]{1,0:T(8,128)(2,1)} %qt_ref.1, bf16[256,1280]{1,0:T(8,128)(2,1)} %k_ref.1, bf16[256,1280]{1,0:T(8,128)(2,1)} %kt_ref.1, bf16[256,1280]{1,0:T(8,128)(2,1)} %v_ref.1, bf16[256,1280]{1,0:T(8,128)(2,1)} %vt_ref.1, ...), custom_call_target="tpu_custom_call" | custom-call | tf_op jit(solution)/shard_map/exchange/pallas_call | solution.py:384
  122.6 0.0 copy-start
  122.6 2.0 %copy.11 = bf16[256,1280]{1,0:T(8,128)(2,1)} copy(bf16[256,1280]{1,0:T(8,128)(2,1)} %get-tuple-element.4) | data formatting | bytes 1310720
  124.6 0.0 copy-done
  124.6 0.8 copy.12
Async XLA Ops:
  122.6 2.0 %copy-start = (bf16[256,1280]{1,0:T(8,128)(2,1)S(1)}, bf16[256,1280]{1,0:T(8,128)(2,1)}, u32[]{:S(2)}) copy-start(bf16[256,1280]{1,0:T(8,128)(2,1)} %get-tuple-element.5) | copy-start | bytes 1966084
where the time goes:
time: 126 us; the launch traced here: 125 us
  Pallas kernels  122 us (97%)
  local copies, waits for them, and re-layouts  2.87 us (2%)
    pallas_call x1, Pallas kernels, exchanged(): pl.pallas_call(functools.partial(exchange_kernel, n), out_shape=[jax.Shap...  122 us
    unnamed x4, local copies, waits for them, and re-layouts  2.87 us

commit v1 on v0

--- a/solution.py
+++ b/solution.py
@@ -146,6 +146,7 @@
     return finish(accumulators)
 
 
+ORDER = [('M', 0), ('B', 0), ('X', 0), ('M', 1), ('X', 1), ('M', 2), ('X', 2), ('M', 3), ('X', 3), ('X', 4), ('X', 5), ('M', 4), ('M', 5)]
 LOG2E = 1.4426950408889634
 MESH = pl.DeviceIdType.MESH
 
@@ -248,46 +249,57 @@
     def lane(i):
         return pl.ds(i * d, d)
 
-    def main_send(refs, buf, send_sem, recv_sem, target):
-        for i, ref in enumerate(refs):
-            send(ref.at[:, cols(target)], buf.at[me, :, lane(i)], send_sem.at[target], recv_sem.at[me], target)
-
-    def main_keep(refs, buf, recv_sem):
-        for i, ref in enumerate(refs):
-            pltpu.make_async_copy(ref.at[:, cols(me)], buf.at[me, :, lane(i)], recv_sem.at[me]).start()
-
-    def extra_send(refs, buf, slot, send_sem, recv_sem, which_side, e):
+    def extra_send(ref, i, buf, slot, send_sem, recv_sem, which_side, e):
         target = host(which_side, e)
 
         @pl.when(target != me)
         def _():
-            for i, ref in enumerate(refs):
-                send(ref.at[:, cols(n + e)], buf.at[slot, :, lane(i)], send_sem, recv_sem.at[slot], target)
+            send(ref.at[:, cols(n + e)], buf.at[slot, :, lane(i)], send_sem, recv_sem.at[slot], target)
 
         @pl.when(target == me)
         def _():
-            for i, ref in enumerate(refs):
-                pltpu.make_async_copy(ref.at[:, cols(n + e)], buf.at[slot, :, lane(i)], recv_sem.at[slot]).start()
-
-    across = [(1 - side) * half + lax.rem(place + i, half) for i in range(half)]
-    beside = [side * half + lax.rem(place + i, half) for i in range(1, half)]
+            pltpu.make_async_copy(ref.at[:, cols(n + e)], buf.at[slot, :, lane(i)], recv_sem.at[slot]).start()
+
+    spread = sorted(range(1, n), key=lambda k: (abs(k - half), k))
+    ring = [lax.rem(me + k, n) for k in spread]
+    def main_one(i, target):
+        ref = (packs + pair)[i]
+        buf, send_sem, recv_sem, at = (kv_buf, kv_send, kv_recv, i) if i < 4 else (q_buf, q_send, q_recv, i - 4)
+        send(ref.at[:, cols(target)], buf.at[me, :, lane(at)], send_sem.at[target], recv_sem.at[me], target)
+
+    def extra_one(i, k, e):
+        if i < 4:
+            extra_send(packs[i], i, xkv_buf, me, xkv_send.at[k, e], xkv_recv, side if k else 1 - side, e)
+        elif k:
+            extra_send(pair[i - 4], i - 4, xq_buf, place, xq_send.at[e], xq_recv, side, e)
 
     turns = [lax.rem(me + e, extra) for e in range(extra)]
-    for e in turns:
-        extra_send(packs, xkv_buf, me, xkv_send.at[0, e], xkv_recv, 1 - side, e)
-    for e in turns:
-        extra_send(packs, xkv_buf, me, xkv_send.at[1, e], xkv_recv, side, e)
-        extra_send(pair, xq_buf, place, xq_send.at[e], xq_recv, side, e)
-    for target in across + beside:
-        send(bias_ref, bias_buf.at[me], b_send.at[target], b_recv.at[me], target)
-    pltpu.make_async_copy(bias_ref, bias_buf.at[me], b_recv.at[me]).start()
-    mixed = [t for two in zip(across, beside) for t in two] + across[len(beside) :]
-    for target in mixed:
-        main_send(packs, kv_buf, kv_send, kv_recv, target)
-    main_keep(packs, kv_buf, kv_recv)
-    for target in mixed:
-        main_send(pair, q_buf, q_send, q_recv, target)
-    main_keep(pair, q_buf, q_recv)
+    for token, i in ORDER:
+        if token == "M":
+            for target in ring:
+                main_one(i, target)
+        elif token == "Q":
+            for target in ring:
+                main_one(4, target)
+                main_one(5, target)
+        elif token == "X":
+            for k in (0, 1):
+                for e in turns:
+                    extra_one(i, k, e)
+        elif token == "C":
+            for e in turns:
+                extra_one(i, 0, e)
+        elif token == "L":
+            for e in turns:
+                extra_one(i, 1, e)
+        elif token == "B":
+            for target in ring:
+                send(bias_ref, bias_buf.at[me], b_send.at[target], b_recv.at[me], target)
+            pltpu.make_async_copy(bias_ref, bias_buf.at[me], b_recv.at[me]).start()
+            for i, ref in enumerate(packs):
+                pltpu.make_async_copy(ref.at[:, cols(me)], kv_buf.at[me, :, lane(i)], kv_recv.at[me]).start()
+            for i, ref in enumerate(pair):
+                pltpu.make_async_copy(ref.at[:, cols(me)], q_buf.at[me, :, lane(i)], q_recv.at[me]).start()
 
     def each(low, high, step):
         def run(i, carried):
@@ -323,15 +335,15 @@
             output, tangent = attend(shard, i, n, xq_buf, xkv_buf, bias_buf, s_buf)
             xout_buf[i, :, 0:d] = output
             xout_buf[i, :, d : 2 * d] = tangent
+            put(xout_buf, i, xo_send, xo_recv, mine, n + mine, shard)
 
         each(0, half, step)
-        each(0, half, lambda i: put(xout_buf, i, xo_send, xo_recv, mine, n + mine, side * half + i))
 
     each(0, n, lambda i: wait(kv_buf.at[i], kv_recv.at[i]))
 
     def order(i):
-        turn = i // half
-        return lax.rem(side + turn, 2) * half + lax.rem(place + n - i, half)
+        ahead = (i + 1) // 2
+        return lax.rem(me + half + n + ahead * (1 - 2 * lax.rem(i, 2)), n)
 
     def main_step(i):
         shard = order(i)
@@ -374,6 +386,17 @@
         each(0, half, step)
 
 
+def store_kernel(a_ref, b_ref, o_ref, ot_ref, sems):
+    moves = [
+        pltpu.make_async_copy(a_ref, o_ref, sems.at[0]),
+        pltpu.make_async_copy(b_ref, ot_ref, sems.at[1]),
+    ]
+    for move in moves:
+        move.start()
+    for move in moves:
+        move.wait()
+
+
 def exchanged(n, queries, query_tangents, keys, key_tangents, values, value_tangents, selection):
     rows, width = queries.shape
     half, extra, d = n // 2, HEADS - n, HEAD_DIM
@@ -381,11 +404,11 @@
     dma = pltpu.SemaphoreType.DMA
     reach = 2 * REACH + 1
     bf = jnp.bfloat16
-    return pl.pallas_call(
+    landed = pl.pallas_call(
         functools.partial(exchange_kernel, n),
-        out_shape=[jax.ShapeDtypeStruct((rows, width), bf)] * 2,
+        out_shape=[vm((rows, width), bf)] * 2,
         in_specs=[pl.BlockSpec(memory_space=pl.ANY)] * 7,
-        out_specs=[pl.BlockSpec(memory_space=pl.ANY)] * 2,
+        out_specs=[pl.BlockSpec(memory_space=vm)] * 2,
         scratch_shapes=[
             vm((n, rows, 2 * d), bf),
             vm((n, rows, 4 * d), bf),
@@ -399,10 +422,18 @@
             dma((n,)), dma((n,)), dma((n,)), dma((n,)), dma((n,)), dma((half,)), dma((extra,)),
         ],
         compiler_params=pltpu.CompilerParams(
-            collective_id=0, has_side_effects=True, vmem_limit_bytes=67_043_328
+            collective_id=0, has_side_effects=True, vmem_limit_bytes=67_043_328 - 4 * rows * width - 131_072
         ),
         name="exchange",
     )(queries, query_tangents, keys, key_tangents, values, value_tangents, selection)
+    return pl.pallas_call(
+        store_kernel,
+        out_shape=[jax.ShapeDtypeStruct((rows, width), bf)] * 2,
+        in_specs=[pl.BlockSpec(memory_space=vm)] * 2,
+        out_specs=[pl.BlockSpec(memory_space=pl.ANY)] * 2,
+        scratch_shapes=[dma((2,))],
+        name="store",
+    )(*[pltpu.with_memory_space_constraint(x, vm) for x in landed])
 
 
 def solution(mesh):

time: 126 us -> 121 us (0.960)
  Pallas kernels: 122 us -> 119 us
  local copies, waits for them, and re-layouts: 2.87 us -> 0 us
    unnamed x4 -> x0, local copies, waits for them, and re-layouts: 2.87 us -> none
    pallas_call x1 -> x2, Pallas kernels: 122 us -> 119 us  [the longest x1 118 us: exchanged(): pl.pallas_call(functools.partial(exchange_kernel, n), out_shape=[vm((rows...]
where the time goes in v1:
time: 121 us; the launch traced here: 120 us
  Pallas kernels  119 us (98%)
    pallas_call x1, Pallas kernels, exchanged(): pl.pallas_call(functools.partial(exchange_kernel, n), out_shape=[vm((rows...  118 us

profile of v1, /device:TPU:10, one launch (start us, length us, event | category | flops | bytes accessed | tf_op | source)
XLA Modules:
  0.0 120.0 jit_solution(10085020631040410180)
XLA Ops:
  0.6 118.3 %exchange.1 = (bf16[256,1280]{1,0:T(8,128)(2,1)S(1)}, bf16[256,1280]{1,0:T(8,128)(2,1)S(1)}) custom-call(bf16[256,1280]{1,0:T(8,128)(2,1)} %q_ref.1, bf16[256,1280]{1,0:T(8,128)(2,1)} %qt_ref.1, bf16[256,1280]{1,0:T(8,128)(2,1)} %k_ref.1, bf16[256,1280]{1,0:T(8,128)(2,1)} %kt_ref.1, bf16[256,1280]{1,0:T(8,128)(2,1)} %v_ref.1, bf16[256,1280]{1,0:T(8,128)(2,1)} %vt_ref.1, ...), custom_call_target="tpu_custom_call" | custom-call | tf_op jit(solution)/shard_map/exchange/pallas_call | solution.py:407
  118.9 1.1 store.1

commit v2 on v1

--- a/solution.py
+++ b/solution.py
@@ -147,6 +147,7 @@
 
 
 ORDER = [('M', 0), ('B', 0), ('X', 0), ('M', 1), ('X', 1), ('M', 2), ('X', 2), ('M', 3), ('X', 3), ('X', 4), ('X', 5), ('M', 4), ('M', 5)]
+HEAD_START = 3
 LOG2E = 1.4426950408889634
 MESH = pl.DeviceIdType.MESH
 
@@ -211,7 +212,7 @@
     n, q_ref, qt_ref, k_ref, kt_ref, v_ref, vt_ref, bias_ref, o_ref, ot_ref,
     q_buf, kv_buf, xq_buf, xkv_buf, bias_buf, out_buf, xout_buf, s_buf,
     kv_send, q_send, b_send, o_send, xkv_send, xq_send, xo_send,
-    kv_recv, q_recv, b_recv, o_recv, xkv_recv, xq_recv, xo_recv,
+    kv_recv, q_recv, b_recv, o_recv, xkv_recv, xq_recv, xo_recv, greet_sem,
 ):
     d = HEAD_DIM
     half = n // 2
@@ -227,12 +228,28 @@
     def host(which_side, e):
         return first_host + which_side * extra + e
 
-    barrier = pltpu.get_barrier_semaphore()
-    for i in range(1, n):
-        pl.semaphore_signal(
-            barrier, inc=1, device_id={"ctx": lax.rem(me + i, n)}, device_id_type=MESH
-        )
-    pl.semaphore_wait(barrier, n - 1)
+    row, rows, y = me // 2, n // 2, lax.rem(me, 2)
+    beside = 2 * row + 1 - y
+    always = me >= 0
+
+    def rows_away(by, column):
+        return [(row + by < rows, 2 * (row + by) + column), (row >= by, 2 * (row - by) + column)]
+
+    adjacent = [(always, beside)] + rows_away(1, y)
+    second = rows_away(2, y) + rows_away(1, 1 - y)
+
+    def greet(sem, group):
+        count = jnp.int32(0)
+        for there, target in group:
+            count = count + there.astype(jnp.int32)
+
+            @pl.when(there)
+            def _():
+                pl.semaphore_signal(sem, inc=1, device_id={"ctx": target}, device_id_type=MESH)
+
+        pl.semaphore_wait(sem, count)
+
+    greet(pltpu.get_barrier_semaphore(), adjacent)
 
     def send(src, dst, send_sem, recv_sem, target):
         pltpu.make_async_remote_copy(
@@ -254,18 +271,18 @@
 
         @pl.when(target != me)
         def _():
-            send(ref.at[:, cols(n + e)], buf.at[slot, :, lane(i)], send_sem, recv_sem.at[slot], target)
+            send(ref.at[:, cols(n + e)], buf.at[slot, :, lane(i)], send_sem, recv_sem, target)
 
         @pl.when(target == me)
         def _():
-            pltpu.make_async_copy(ref.at[:, cols(n + e)], buf.at[slot, :, lane(i)], recv_sem.at[slot]).start()
+            pltpu.make_async_copy(ref.at[:, cols(n + e)], buf.at[slot, :, lane(i)], recv_sem).start()
 
     spread = sorted(range(1, n), key=lambda k: (abs(k - half), k))
     ring = [lax.rem(me + k, n) for k in spread]
     def main_one(i, target):
         ref = (packs + pair)[i]
-        buf, send_sem, recv_sem, at = (kv_buf, kv_send, kv_recv, i) if i < 4 else (q_buf, q_send, q_recv, i - 4)
-        send(ref.at[:, cols(target)], buf.at[me, :, lane(at)], send_sem.at[target], recv_sem.at[me], target)
+        buf, send_sem, recv_sem, at = (kv_buf, kv_send, kv_recv, i) if i < 4 else (q_buf, q_send, q_recv.at[me], i - 4)
+        send(ref.at[:, cols(target)], buf.at[me, :, lane(at)], send_sem, recv_sem, target)
 
     def extra_one(i, k, e):
         if i < 4:
@@ -273,31 +290,37 @@
         elif k:
             extra_send(pair[i - 4], i - 4, xq_buf, place, xq_send.at[e], xq_recv, side, e)
 
+    for i in range(HEAD_START):
+        for there, target in adjacent:
+            @pl.when(there)
+            def _():
+                main_one(i, target)
+
+    greet(greet_sem.at[0], adjacent)
+    greet(greet_sem.at[1], second)
+
     turns = [lax.rem(me + e, extra) for e in range(extra)]
     for token, i in ORDER:
         if token == "M":
             for target in ring:
-                main_one(i, target)
-        elif token == "Q":
-            for target in ring:
-                main_one(4, target)
-                main_one(5, target)
+                if i < HEAD_START:
+                    near = functools.reduce(jnp.logical_or, [jnp.logical_and(there, t == target) for there, t in adjacent])
+
+                    @pl.when(jnp.logical_not(near))
+                    def _():
+                        main_one(i, target)
+                else:
+                    main_one(i, target)
         elif token == "X":
             for k in (0, 1):
                 for e in turns:
                     extra_one(i, k, e)
-        elif token == "C":
-            for e in turns:
-                extra_one(i, 0, e)
-        elif token == "L":
-            for e in turns:
-                extra_one(i, 1, e)
         elif token == "B":
             for target in ring:
-                send(bias_ref, bias_buf.at[me], b_send.at[target], b_recv.at[me], target)
-            pltpu.make_async_copy(bias_ref, bias_buf.at[me], b_recv.at[me]).start()
+                send(bias_ref, bias_buf.at[me], b_send, b_recv, target)
+            pltpu.make_async_copy(bias_ref, bias_buf.at[me], b_recv).start()
             for i, ref in enumerate(packs):
-                pltpu.make_async_copy(ref.at[:, cols(me)], kv_buf.at[me, :, lane(i)], kv_recv.at[me]).start()
+                pltpu.make_async_copy(ref.at[:, cols(me)], kv_buf.at[me, :, lane(i)], kv_recv).start()
             for i, ref in enumerate(pair):
                 pltpu.make_async_copy(ref.at[:, cols(me)], q_buf.at[me, :, lane(i)], q_recv.at[me]).start()
 
@@ -308,38 +331,38 @@
 
         lax.fori_loop(low, high, run, 0)
 
-    each(0, n, lambda i: wait(bias_buf.at[i], b_recv.at[i]))
+    wait(bias_buf, b_recv)
 
     is_host = jnp.logical_and(me >= first_host, me < first_host + 2 * extra)
     mine = lax.rem(me - first_host + n * extra, extra)
     outs = (o_ref, ot_ref)
 
-    def put(buf, slot, send_sem, recv_sem, source, head, target):
+    def put(buf, slot, send_sem, recv_sem, head, target):
         @pl.when(target != me)
         def _():
             for i, ref in enumerate(outs):
-                send(buf.at[slot, :, lane(i)], ref.at[:, cols(head)], send_sem.at[slot], recv_sem.at[source], target)
+                send(buf.at[slot, :, lane(i)], ref.at[:, cols(head)], send_sem, recv_sem, target)
 
         @pl.when(target == me)
         def _():
             for i, ref in enumerate(outs):
-                pltpu.make_async_copy(buf.at[slot, :, lane(i)], ref.at[:, cols(head)], recv_sem.at[source]).start()
+                pltpu.make_async_copy(buf.at[slot, :, lane(i)], ref.at[:, cols(head)], recv_sem).start()
 
     @pl.when(is_host)
     def _():
-        each(0, n, lambda i: wait(xkv_buf.at[i], xkv_recv.at[i]))
-        each(0, half, lambda i: wait(xq_buf.at[i], xq_recv.at[i]))
+        wait(xkv_buf, xkv_recv)
+        wait(xq_buf, xq_recv)
 
         def step(i):
             shard = side * half + i
             output, tangent = attend(shard, i, n, xq_buf, xkv_buf, bias_buf, s_buf)
             xout_buf[i, :, 0:d] = output
             xout_buf[i, :, d : 2 * d] = tangent
-            put(xout_buf, i, xo_send, xo_recv, mine, n + mine, shard)
+            put(xout_buf, i, xo_send, xo_recv, n + mine, shard)
 
         each(0, half, step)
 
-    each(0, n, lambda i: wait(kv_buf.at[i], kv_recv.at[i]))
+    wait(kv_buf, kv_recv)
 
     def order(i):
         ahead = (i + 1) // 2
@@ -351,21 +374,14 @@
         output, tangent = attend(shard, shard, n, q_buf, kv_buf, bias_buf, s_buf)
         out_buf[shard, :, 0:d] = output
         out_buf[shard, :, d : 2 * d] = tangent
-        put(out_buf, shard, o_send, o_recv, me, me, shard)
+        put(out_buf, shard, o_send, o_recv, me, shard)
 
     each(0, n, main_step)
 
-    each(0, n, lambda i: wait(out_buf.at[i], o_recv.at[i]))
-    each(0, extra, lambda i: wait(xout_buf.at[i], xo_recv.at[i]))
-
-    def drain(i):
-        target = lax.rem(me + i, n)
-        wait(kv_buf.at[target], kv_send.at[target])
-        wait(q_buf.at[target], q_send.at[target])
-        wait(bias_buf.at[target], b_send.at[target])
-        wait(out_buf.at[target], o_send.at[target])
-
-    each(1, n, drain)
+    others = pl.ds(0, n - 1)
+    wait(kv_buf.at[others], kv_send)
+    wait(q_buf.at[others], q_send)
+    wait(bias_buf.at[others], b_send)
     for e in range(extra):
         @pl.when(host(1 - side, e) != me)
         def _():
@@ -378,12 +394,11 @@
 
     @pl.when(is_host)
     def _():
-        def step(i):
-            @pl.when(side * half + i != me)
-            def _():
-                wait(xout_buf.at[i], xo_send.at[i])
-
-        each(0, half, step)
+        wait(xout_buf.at[pl.ds(0, half - 1)], xo_send)
+
+    wait(xout_buf.at[pl.ds(0, extra)], xo_recv)
+    wait(out_buf, o_recv)
+    wait(out_buf.at[others], o_send)
 
 
 def store_kernel(a_ref, b_ref, o_ref, ot_ref, sems):
@@ -418,8 +433,9 @@
             vm((n, rows, 2 * d), bf),
             vm((half, rows, 2 * d), bf),
             vm((reach, rows, rows), jnp.float32),
-            dma((n,)), dma((n,)), dma((n,)), dma((n,)), dma((2, extra)), dma((extra,)), dma((half,)),
-            dma((n,)), dma((n,)), dma((n,)), dma((n,)), dma((n,)), dma((half,)), dma((extra,)),
+            dma, dma, dma, dma, dma((2, extra)), dma((extra,)), dma,
+            dma, dma((n,)), dma, dma, dma, dma, dma,
+            pltpu.SemaphoreType.REGULAR((2,)),
         ],
         compiler_params=pltpu.CompilerParams(
             collective_id=0, has_side_effects=True, vmem_limit_bytes=67_043_328 - 4 * rows * width - 131_072

time: 121 us -> 119 us (0.983)
  Pallas kernels: 119 us -> 117 us
    pallas_call x1, Pallas kernels: 118 us -> 116 us  [exchanged(): pl.pallas_call(functools.partial(exchange_kernel, n), out_shape=[vm((rows...]
where the time goes in v2:
time: 119 us; the launch traced here: 118 us
  Pallas kernels  117 us (98%)
    pallas_call x1, Pallas kernels, exchanged(): pl.pallas_call(functools.partial(exchange_kernel, n), out_shape=[vm((rows...  116 us

profile of v2, /device:TPU:10, one launch (start us, length us, event | category | flops | bytes accessed | tf_op | source)
XLA Modules:
  0.0 117.9 jit_solution(8355501813366331862)
XLA Ops:
  0.6 116.2 %exchange.1 = (bf16[256,1280]{1,0:T(8,128)(2,1)S(1)}, bf16[256,1280]{1,0:T(8,128)(2,1)S(1)}) custom-call(bf16[256,1280]{1,0:T(8,128)(2,1)} %q_ref.1, bf16[256,1280]{1,0:T(8,128)(2,1)} %qt_ref.1, bf16[256,1280]{1,0:T(8,128)(2,1)} %k_ref.1, bf16[256,1280]{1,0:T(8,128)(2,1)} %kt_ref.1, bf16[256,1280]{1,0:T(8,128)(2,1)} %v_ref.1, bf16[256,1280]{1,0:T(8,128)(2,1)} %vt_ref.1, ...), custom_call_target="tpu_custom_call" | custom-call | tf_op jit(solution)/shard_map/exchange/pallas_call | solution.py:422
  116.8 1.1 store.1

commit v3 on v2

--- a/solution.py
+++ b/solution.py
@@ -229,27 +229,22 @@
         return first_host + which_side * extra + e
 
     row, rows, y = me // 2, n // 2, lax.rem(me, 2)
+    is_inner = jnp.logical_and(row > 0, row < rows - 1)
     beside = 2 * row + 1 - y
-    always = me >= 0
-
-    def rows_away(by, column):
-        return [(row + by < rows, 2 * (row + by) + column), (row >= by, 2 * (row - by) + column)]
-
-    adjacent = [(always, beside)] + rows_away(1, y)
-    second = rows_away(2, y) + rows_away(1, 1 - y)
-
-    def greet(sem, group):
-        count = jnp.int32(0)
-        for there, target in group:
-            count = count + there.astype(jnp.int32)
-
-            @pl.when(there)
-            def _():
-                pl.semaphore_signal(sem, inc=1, device_id={"ctx": target}, device_id_type=MESH)
-
-        pl.semaphore_wait(sem, count)
-
-    greet(pltpu.get_barrier_semaphore(), adjacent)
+    partner = 2 * (rows - 1 - row) + y
+    along = 2 * jnp.where(row % 2 == 0, row + 1, row - 1) + y
+    barrier = pltpu.get_barrier_semaphore()
+
+    def signal(sem, target):
+        pl.semaphore_signal(sem, inc=1, device_id={"ctx": target}, device_id_type=MESH)
+
+    signal(barrier, jnp.where(is_inner, partner, beside))
+
+    @pl.when(is_inner)
+    def _():
+        signal(barrier, along)
+
+    pl.semaphore_wait(barrier, jnp.where(is_inner, 1, 2))
 
     def send(src, dst, send_sem, recv_sem, target):
         pltpu.make_async_remote_copy(
@@ -290,21 +285,34 @@
         elif k:
             extra_send(pair[i - 4], i - 4, xq_buf, place, xq_send.at[e], xq_recv, side, e)
 
-    for i in range(HEAD_START):
-        for there, target in adjacent:
-            @pl.when(there)
-            def _():
+    def head_start(*targets):
+        for i in range(HEAD_START):
+            for target in targets:
                 main_one(i, target)
 
-    greet(greet_sem.at[0], adjacent)
-    greet(greet_sem.at[1], second)
+    @pl.when(is_inner)
+    def _():
+        head_start(partner)
+        pl.semaphore_wait(greet_sem.at[0], 1)
+        signal(greet_sem.at[1], partner)
+        head_start(along, beside)
+        pl.semaphore_wait(greet_sem.at[1], 1)
+        signal(greet_sem.at[1], along)
+
+    @pl.when(jnp.logical_not(is_inner))
+    def _():
+        signal(greet_sem.at[0], beside)
+        head_start(along, beside)
+        pl.semaphore_wait(greet_sem.at[0], 1)
+        signal(greet_sem.at[0], along)
+        pl.semaphore_wait(greet_sem.at[1], 1)
 
     turns = [lax.rem(me + e, extra) for e in range(extra)]
     for token, i in ORDER:
         if token == "M":
             for target in ring:
                 if i < HEAD_START:
-                    near = functools.reduce(jnp.logical_or, [jnp.logical_and(there, t == target) for there, t in adjacent])
+                    near = functools.reduce(jnp.logical_or, [target == along, target == beside, jnp.logical_and(is_inner, target == partner)])
 
                     @pl.when(jnp.logical_not(near))
                     def _():

time: 119 us -> 118 us (level)
    pallas_call x1, Pallas kernels: 116 us -> 115 us  [exchanged(): pl.pallas_call(functools.partial(exchange_kernel, n), out_shape=[vm((rows...]
where the time goes in v3:
time: 118 us; the launch traced here: 116 us
  Pallas kernels  116 us (98%)
    pallas_call x1, Pallas kernels, exchanged(): pl.pallas_call(functools.partial(exchange_kernel, n), out_shape=[vm((rows...  115 us

profile of v3, /device:TPU:10, one launch (start us, length us, event | category | flops | bytes accessed | tf_op | source)
XLA Modules:
  0.0 116.5 jit_solution(16120502530533617059)
XLA Ops:
  0.6 114.8 %exchange.1 = (bf16[256,1280]{1,0:T(8,128)(2,1)S(1)}, bf16[256,1280]{1,0:T(8,128)(2,1)S(1)}) custom-call(bf16[256,1280]{1,0:T(8,128)(2,1)} %q_ref.1, bf16[256,1280]{1,0:T(8,128)(2,1)} %qt_ref.1, bf16[256,1280]{1,0:T(8,128)(2,1)} %k_ref.1, bf16[256,1280]{1,0:T(8,128)(2,1)} %kt_ref.1, bf16[256,1280]{1,0:T(8,128)(2,1)} %v_ref.1, bf16[256,1280]{1,0:T(8,128)(2,1)} %vt_ref.1, ...), custom_call_target="tpu_custom_call" | custom-call | tf_op jit(solution)/shard_map/exchange/pallas_call | solution.py:430
  115.4 1.1 store.1

commit v4 on v3

--- a/solution.py
+++ b/solution.py
@@ -148,6 +148,9 @@
 
 ORDER = [('M', 0), ('B', 0), ('X', 0), ('M', 1), ('X', 1), ('M', 2), ('X', 2), ('M', 3), ('X', 3), ('X', 4), ('X', 5), ('M', 4), ('M', 5)]
 HEAD_START = 3
+STEPS = [(2, 0), (2, 1), (1, 1), (1, 0), (3, 1), (3, 0), (0, 1)]
+INNER = [5, 4, 6, 7, 0, 1, 2, 3]
+OUTER = [3, 2, 6, 7, 4, 5, 0, 1]
 LOG2E = 1.4426950408889634
 MESH = pl.DeviceIdType.MESH
 
@@ -272,8 +275,11 @@
         def _():
             pltpu.make_async_copy(ref.at[:, cols(n + e)], buf.at[slot, :, lane(i)], recv_sem).start()
 
-    spread = sorted(range(1, n), key=lambda k: (abs(k - half), k))
-    ring = [lax.rem(me + k, n) for k in spread]
+    toward = 1 - 2 * side
+    ring = [
+        2 * lax.rem(row + toward * dz + rows, rows) + (1 - y if dy else y) for dz, dy in STEPS
+    ]
+
     def main_one(i, target):
         ref = (packs + pair)[i]
         buf, send_sem, recv_sem, at = (kv_buf, kv_send, kv_recv, i) if i < 4 else (q_buf, q_send, q_recv.at[me], i - 4)
@@ -373,8 +379,11 @@
     wait(kv_buf, kv_recv)
 
     def order(i):
-        ahead = (i + 1) // 2
-        return lax.rem(me + half + n + ahead * (1 - 2 * lax.rem(i, 2)), n)
+        shard = me
+        for k, (at_inner, at_outer) in enumerate(zip(INNER, OUTER)):
+            target = jnp.where(is_inner, (*ring, me)[at_inner], (*ring, me)[at_outer])
+            shard = jnp.where(i == k, target, shard)
+        return shard
 
     def main_step(i):
         shard = order(i)
@@ -405,8 +414,8 @@
         wait(xout_buf.at[pl.ds(0, half - 1)], xo_send)
 
     wait(xout_buf.at[pl.ds(0, extra)], xo_recv)
+    wait(out_buf.at[others], o_send)
     wait(out_buf, o_recv)
-    wait(out_buf.at[others], o_send)
 
 
 def store_kernel(a_ref, b_ref, o_ref, ot_ref, sems):

time: 118 us -> 118 us (level)
  no operation moved by 1% of the time
where the time goes in v4:
time: 118 us; the launch traced here: 117 us
  Pallas kernels  117 us (99%)
    pallas_call x1, Pallas kernels, exchanged(): pl.pallas_call(functools.partial(exchange_kernel, n), out_shape=[vm((rows...  116 us

profile of v4, /device:TPU:10, one launch (start us, length us, event | category | flops | bytes accessed | tf_op | source)
XLA Modules:
  0.0 117.3 jit_solution(12303547608314292988)
XLA Ops:
  0.6 115.5 %exchange.1 = (bf16[256,1280]{1,0:T(8,128)(2,1)S(1)}, bf16[256,1280]{1,0:T(8,128)(2,1)S(1)}) custom-call(bf16[256,1280]{1,0:T(8,128)(2,1)} %q_ref.1, bf16[256,1280]{1,0:T(8,128)(2,1)} %qt_ref.1, bf16[256,1280]{1,0:T(8,128)(2,1)} %k_ref.1, bf16[256,1280]{1,0:T(8,128)(2,1)} %kt_ref.1, bf16[256,1280]{1,0:T(8,128)(2,1)} %v_ref.1, bf16[256,1280]{1,0:T(8,128)(2,1)} %vt_ref.1, ...), custom_call_target="tpu_custom_call" | custom-call | tf_op jit(solution)/shard_map/exchange/pallas_call | solution.py:439
  116.2 1.1 store.1

commit v5 on v4

--- a/solution.py
+++ b/solution.py
@@ -146,7 +146,7 @@
     return finish(accumulators)
 
 
-ORDER = [('M', 0), ('B', 0), ('X', 0), ('M', 1), ('X', 1), ('M', 2), ('X', 2), ('M', 3), ('X', 3), ('X', 4), ('X', 5), ('M', 4), ('M', 5)]
+ORDER = [('M', 0), ('B', 0), ('X', 0), ('X', 1), ('X', 2), ('X', 3), ('X', 4), ('X', 5), ('M', 1), ('M', 2), ('M', 3), ('M', 4), ('M', 5)]
 HEAD_START = 3
 STEPS = [(2, 0), (2, 1), (1, 1), (1, 0), (3, 1), (3, 0), (0, 1)]
 INNER = [5, 4, 6, 7, 0, 1, 2, 3]

time: 118 us -> 117 us (level)
  no operation moved by 1% of the time
where the time goes in v5:
time: 117 us
  Pallas kernels  117 us (100%)
    pallas_call x1, Pallas kernels, exchanged(): pl.pallas_call(functools.partial(exchange_kernel, n), out_shape=[vm((rows...  116 us

profile of v5, /device:TPU:10, one launch (start us, length us, event | category | flops | bytes accessed | tf_op | source)
XLA Modules:
  0.0 117.3 jit_solution(589788158689162063)
XLA Ops:
  0.6 115.6 %exchange.1 = (bf16[256,1280]{1,0:T(8,128)(2,1)S(1)}, bf16[256,1280]{1,0:T(8,128)(2,1)S(1)}) custom-call(bf16[256,1280]{1,0:T(8,128)(2,1)} %q_ref.1, bf16[256,1280]{1,0:T(8,128)(2,1)} %qt_ref.1, bf16[256,1280]{1,0:T(8,128)(2,1)} %k_ref.1, bf16[256,1280]{1,0:T(8,128)(2,1)} %kt_ref.1, bf16[256,1280]{1,0:T(8,128)(2,1)} %v_ref.1, bf16[256,1280]{1,0:T(8,128)(2,1)} %vt_ref.1, ...), custom_call_target="tpu_custom_call" | custom-call | tf_op jit(solution)/shard_map/exchange/pallas_call | solution.py:439
  116.2 1.1 store.1

commit v6 on v5

--- a/solution.py
+++ b/solution.py
@@ -146,9 +146,9 @@
     return finish(accumulators)
 
 
-ORDER = [('M', 0), ('B', 0), ('X', 0), ('X', 1), ('X', 2), ('X', 3), ('X', 4), ('X', 5), ('M', 1), ('M', 2), ('M', 3), ('M', 4), ('M', 5)]
+ORDER = [('M', 0), ('X', 0), ('X', 1), ('X', 2), ('X', 3), ('X', 4), ('X', 5), ('B', 0), ('M', 1), ('M', 2), ('M', 3), ('M', 4), ('M', 5)]
 HEAD_START = 3
-STEPS = [(2, 0), (2, 1), (1, 1), (1, 0), (3, 1), (3, 0), (0, 1)]
+STEPS = [(2, 1), (2, 0), (1, 1), (1, 0), (3, 1), (3, 0), (0, 1)]
 INNER = [5, 4, 6, 7, 0, 1, 2, 3]
 OUTER = [3, 2, 6, 7, 4, 5, 0, 1]
 LOG2E = 1.4426950408889634
@@ -287,9 +287,9 @@
 
     def extra_one(i, k, e):
         if i < 4:
-            extra_send(packs[i], i, xkv_buf, me, xkv_send.at[k, e], xkv_recv, side if k else 1 - side, e)
+            extra_send(packs[i], i, xkv_buf, me, xkv_send, xkv_recv, side if k else 1 - side, e)
         elif k:
-            extra_send(pair[i - 4], i - 4, xq_buf, place, xq_send.at[e], xq_recv, side, e)
+            extra_send(pair[i - 4], i - 4, xq_buf, place, xq_send, xq_recv, side, e)
 
     def head_start(*targets):
         for i in range(HEAD_START):
@@ -399,15 +399,15 @@
     wait(kv_buf.at[others], kv_send)
     wait(q_buf.at[others], q_send)
     wait(bias_buf.at[others], b_send)
-    for e in range(extra):
-        @pl.when(host(1 - side, e) != me)
-        def _():
-            wait(xkv_buf.at[0], xkv_send.at[0, e])
-
-        @pl.when(host(side, e) != me)
-        def _():
-            wait(xkv_buf.at[0], xkv_send.at[1, e])
-            wait(xq_buf.at[0], xq_send.at[e])
+    @pl.when(is_host)
+    def _():
+        wait(xkv_buf.at[pl.ds(0, 2 * extra - 1)], xkv_send)
+        wait(xq_buf.at[pl.ds(0, extra - 1)], xq_send)
+
+    @pl.when(jnp.logical_not(is_host))
+    def _():
+        wait(xkv_buf.at[pl.ds(0, 2 * extra)], xkv_send)
+        wait(xq_buf.at[pl.ds(0, extra)], xq_send)
 
     @pl.when(is_host)
     def _():
@@ -450,7 +450,7 @@
             vm((n, rows, 2 * d), bf),
             vm((half, rows, 2 * d), bf),
             vm((reach, rows, rows), jnp.float32),
-            dma, dma, dma, dma, dma((2, extra)), dma((extra,)), dma,
+            dma, dma, dma, dma, dma, dma, dma,
             dma, dma((n,)), dma, dma, dma, dma, dma,
             pltpu.SemaphoreType.REGULAR((2,)),
         ],

time: 117 us -> 117 us (level)
  no operation moved by 1% of the time
where the time goes in v6:
time: 117 us
  Pallas kernels  117 us (100%)
    pallas_call x1, Pallas kernels, exchanged(): pl.pallas_call(functools.partial(exchange_kernel, n), out_shape=[vm((rows...  116 us

profile of v6, /device:TPU:10, one launch (start us, length us, event | category | flops | bytes accessed | tf_op | source)
XLA Modules:
  0.0 117.2 jit_solution(7591204299476710144)
XLA Ops:
  0.6 115.5 %exchange.1 = (bf16[256,1280]{1,0:T(8,128)(2,1)S(1)}, bf16[256,1280]{1,0:T(8,128)(2,1)S(1)}) custom-call(bf16[256,1280]{1,0:T(8,128)(2,1)} %q_ref.1, bf16[256,1280]{1,0:T(8,128)(2,1)} %qt_ref.1, bf16[256,1280]{1,0:T(8,128)(2,1)} %k_ref.1, bf16[256,1280]{1,0:T(8,128)(2,1)} %kt_ref.1, bf16[256,1280]{1,0:T(8,128)(2,1)} %v_ref.1, bf16[256,1280]{1,0:T(8,128)(2,1)} %vt_ref.1, ...), custom_call_target="tpu_custom_call" | custom-call | tf_op jit(solution)/shard_map/exchange/pallas_call | solution.py:439
  116.2 1.1 store.1

commit v7 on v5

--- a/solution.py
+++ b/solution.py
@@ -150,7 +150,7 @@
 HEAD_START = 3
 STEPS = [(2, 0), (2, 1), (1, 1), (1, 0), (3, 1), (3, 0), (0, 1)]
 INNER = [5, 4, 6, 7, 0, 1, 2, 3]
-OUTER = [3, 2, 6, 7, 4, 5, 0, 1]
+OUTER = [3, 2, 6, 7, 0, 1, 4, 5]
 LOG2E = 1.4426950408889634
 MESH = pl.DeviceIdType.MESH
 

time: 117 us -> 117 us (level)
  no operation moved by 1% of the time
where the time goes in v7:
time: 117 us
  Pallas kernels  117 us (100%)
    pallas_call x1, Pallas kernels, exchanged(): pl.pallas_call(functools.partial(exchange_kernel, n), out_shape=[vm((rows...  116 us

profile of v7, /device:TPU:10, one launch (start us, length us, event | category | flops | bytes accessed | tf_op | source)
XLA Modules:
  0.0 117.3 jit_solution(4601846942624981847)
XLA Ops:
  0.6 115.6 %exchange.1 = (bf16[256,1280]{1,0:T(8,128)(2,1)S(1)}, bf16[256,1280]{1,0:T(8,128)(2,1)S(1)}) custom-call(bf16[256,1280]{1,0:T(8,128)(2,1)} %q_ref.1, bf16[256,1280]{1,0:T(8,128)(2,1)} %qt_ref.1, bf16[256,1280]{1,0:T(8,128)(2,1)} %k_ref.1, bf16[256,1280]{1,0:T(8,128)(2,1)} %kt_ref.1, bf16[256,1280]{1,0:T(8,128)(2,1)} %v_ref.1, bf16[256,1280]{1,0:T(8,128)(2,1)} %vt_ref.1, ...), custom_call_target="tpu_custom_call" | custom-call | tf_op jit(solution)/shard_map/exchange/pallas_call | solution.py:439
  116.2 1.1 store.1

commit v8 on v7

--- a/solution.py
+++ b/solution.py
@@ -147,7 +147,7 @@
 
 
 ORDER = [('M', 0), ('B', 0), ('X', 0), ('X', 1), ('X', 2), ('X', 3), ('X', 4), ('X', 5), ('M', 1), ('M', 2), ('M', 3), ('M', 4), ('M', 5)]
-HEAD_START = 3
+HEAD_START = 4
 STEPS = [(2, 0), (2, 1), (1, 1), (1, 0), (3, 1), (3, 0), (0, 1)]
 INNER = [5, 4, 6, 7, 0, 1, 2, 3]
 OUTER = [3, 2, 6, 7, 0, 1, 4, 5]

time: 117 us -> 117 us (level)
  no operation moved by 1% of the time
where the time goes in v8:
time: 117 us
  Pallas kernels  117 us (100%)
    pallas_call x1, Pallas kernels, exchanged(): pl.pallas_call(functools.partial(exchange_kernel, n), out_shape=[vm((rows...  116 us

profile of v8, /device:TPU:10, one launch (start us, length us, event | category | flops | bytes accessed | tf_op | source)
XLA Modules:
  0.0 117.2 jit_solution(382632412612349524)
XLA Ops:
  0.6 115.5 %exchange.1 = (bf16[256,1280]{1,0:T(8,128)(2,1)S(1)}, bf16[256,1280]{1,0:T(8,128)(2,1)S(1)}) custom-call(bf16[256,1280]{1,0:T(8,128)(2,1)} %q_ref.1, bf16[256,1280]{1,0:T(8,128)(2,1)} %qt_ref.1, bf16[256,1280]{1,0:T(8,128)(2,1)} %k_ref.1, bf16[256,1280]{1,0:T(8,128)(2,1)} %kt_ref.1, bf16[256,1280]{1,0:T(8,128)(2,1)} %v_ref.1, bf16[256,1280]{1,0:T(8,128)(2,1)} %vt_ref.1, ...), custom_call_target="tpu_custom_call" | custom-call | tf_op jit(solution)/shard_map/exchange/pallas_call | solution.py:439
  116.2 1.1 store.1

commit v9 on v7

--- a/solution.py
+++ b/solution.py
@@ -149,7 +149,7 @@
 ORDER = [('M', 0), ('B', 0), ('X', 0), ('X', 1), ('X', 2), ('X', 3), ('X', 4), ('X', 5), ('M', 1), ('M', 2), ('M', 3), ('M', 4), ('M', 5)]
 HEAD_START = 3
 STEPS = [(2, 0), (2, 1), (1, 1), (1, 0), (3, 1), (3, 0), (0, 1)]
-INNER = [5, 4, 6, 7, 0, 1, 2, 3]
+INNER = [0, 1, 5, 4, 6, 7, 2, 3]
 OUTER = [3, 2, 6, 7, 0, 1, 4, 5]
 LOG2E = 1.4426950408889634
 MESH = pl.DeviceIdType.MESH

time: 117 us -> 117 us (level)
  no operation moved by 1% of the time
where the time goes in v9:
time: 117 us
  Pallas kernels  117 us (100%)
    pallas_call x1, Pallas kernels, exchanged(): pl.pallas_call(functools.partial(exchange_kernel, n), out_shape=[vm((rows...  116 us

profile of v9, /device:TPU:10, one launch (start us, length us, event | category | flops | bytes accessed | tf_op | source)
XLA Modules:
  0.0 117.3 jit_solution(14702842078160852139)
XLA Ops:
  0.6 115.6 %exchange.1 = (bf16[256,1280]{1,0:T(8,128)(2,1)S(1)}, bf16[256,1280]{1,0:T(8,128)(2,1)S(1)}) custom-call(bf16[256,1280]{1,0:T(8,128)(2,1)} %q_ref.1, bf16[256,1280]{1,0:T(8,128)(2,1)} %qt_ref.1, bf16[256,1280]{1,0:T(8,128)(2,1)} %k_ref.1, bf16[256,1280]{1,0:T(8,128)(2,1)} %kt_ref.1, bf16[256,1280]{1,0:T(8,128)(2,1)} %v_ref.1, bf16[256,1280]{1,0:T(8,128)(2,1)} %vt_ref.1, ...), custom_call_target="tpu_custom_call" | custom-call | tf_op jit(solution)/shard_map/exchange/pallas_call | solution.py:439
  116.2 1.1 store.1
